TPU v7x, 128 devices: a whole 4x4x4 slice. The times are simulated.
128 devices in a mesh: dp: 1, tp: 16 (over z, y), dm: 8 (over x, core).
Axes of the slice: x: 4, y: 4, z: 4, core: 2. Of those that a mesh axis runs over, the one named last changes fastest.
Arguments:
- resid_in: bfloat16 [1536, 3072], P('dp', 'dm')
- k_cache: bfloat16 [1536, 16, 16, 256], P(('dp', 'dm'), 'tp')
- v_cache: bfloat16 [1536, 16, 16, 256], P(('dp', 'dm'), 'tp')
- cache_len: int32 [1536], P('dp')
- norm_attn: bfloat16 [3072], P('dm')
- w_q: bfloat16 [3072, 4096], P('dm', 'tp')
- w_k: bfloat16 [3072, 4096], P('dm', 'tp')
- w_v: bfloat16 [3072, 4096], P('dm', 'tp')
- w_o: bfloat16 [4096, 3072], P('tp', 'dm')
- norm_mlp: bfloat16 [3072], P('dm')
- w_gate: bfloat16 [3072, 24576], P('dm', 'tp')
- w_up: bfloat16 [3072, 24576], P('dm', 'tp')
- w_down: bfloat16 [24576, 3072], P('tp', 'dm')
Outputs:
- output 1: bfloat16 [1536, 3072], P('dp', 'dm')
- output 2: bfloat16 [1536, 16, 16, 256], P(('dp', 'dm'), 'tp')
- output 3: bfloat16 [1536, 16, 16, 256], P(('dp', 'dm'), 'tp')
All inputs are finite; a program needn't handle non-finite values.
Results may differ from a plain program's by a relative error of at most 0.010591.
Values are sent between devices in bfloat16 or wider.
A program may use at most 1 GiB of HBM per device.

v0:
```python
import jax
import jax.numpy as jnp
from jax import lax
from jax.sharding import PartitionSpec as P

EPSILON = 1e-6
ROPE_THETA = 10000.0


def rope_rotate(vectors, positions):
    half_dim = vectors.shape[-1] // 2
    inv_freq = ROPE_THETA ** (-2.0 * jnp.arange(half_dim, dtype=jnp.float32) / vectors.shape[-1])
    angles = positions.astype(jnp.float32)[:, None] * inv_freq[None, :]
    cos_part = jnp.cos(angles)[:, None, :]
    sin_part = jnp.sin(angles)[:, None, :]
    first_half = vectors[..., :half_dim]
    second_half = vectors[..., half_dim:]
    return jnp.concatenate([first_half * cos_part - second_half * sin_part, second_half * cos_part + first_half * sin_part], axis=-1)


def attend(q_rot, k_cache, v_cache, k_new, v_new, lengths):
    slot_ids = jnp.arange(k_cache.shape[2])
    slot_hit = slot_ids[None, :] == lengths[:, None]
    valid_mask = slot_ids[None, :] <= lengths[:, None]
    k_upd = jnp.where(slot_hit[:, None, :, None], k_new[:, :, None, :], k_cache)
    v_upd = jnp.where(slot_hit[:, None, :, None], v_new[:, :, None, :], v_cache)
    scores = jnp.einsum('bhe,bhte->bht', q_rot, k_upd, preferred_element_type=jnp.float32)
    scores = jnp.where(valid_mask[:, None, :], scores, -1e30)
    attn_probs = jax.nn.softmax(scores, axis=-1).astype(jnp.bfloat16)
    attn_out = jnp.einsum('bht,bhte->bhe', attn_probs, v_upd, preferred_element_type=jnp.float32)
    return attn_out.astype(jnp.bfloat16), k_upd, v_upd


def solution(mesh):
    dm_size = mesh.shape['dm']
    cache_spec = P(('dp', 'dm'), 'tp', None, None)
    resid_spec = P('dp', 'dm')
    col_spec = P('dm', 'tp')
    row_spec = P('tp', 'dm')
    in_specs = (resid_spec, cache_spec, cache_spec, P('dp'), P('dm'), col_spec, col_spec, col_spec, row_spec, P('dm'), col_spec, col_spec, row_spec)
    out_specs = (resid_spec, cache_spec, cache_spec)

    def local_step(resid_in, k_cache, v_cache, cache_len, norm_attn, w_q, w_k, w_v, w_o, norm_mlp, w_gate, w_up, w_down):
        batch_rows = resid_in.shape[0]
        row_count = batch_rows // dm_size
        d_model = resid_in.shape[1] * dm_size
        head_count = k_cache.shape[1]
        head_dim = k_cache.shape[3]
        lengths = lax.dynamic_slice_in_dim(cache_len, lax.axis_index('dm') * row_count, row_count)

        def width_norm(rows_f, norm_gain):
            sq_total = lax.psum(jnp.sum(rows_f * rows_f, axis=1, keepdims=True), 'dm')
            inv_rms = lax.rsqrt(sq_total / d_model + EPSILON)
            return (rows_f * inv_rms * (1.0 + norm_gain.astype(jnp.float32))).astype(jnp.bfloat16)

        def row_sum(partial_val):
            summed = lax.psum_scatter(partial_val, 'dm', scatter_dimension=0, tiled=True)
            return summed.reshape(row_count, head_count, head_dim)

        resid_f = resid_in.astype(jnp.float32)
        normed = width_norm(resid_f, norm_attn)
        q_sum = row_sum(jnp.dot(normed, w_q, preferred_element_type=jnp.float32))
        k_sum = row_sum(jnp.dot(normed, w_k, preferred_element_type=jnp.float32))
        v_sum = row_sum(jnp.dot(normed, w_v, preferred_element_type=jnp.float32))
        q_rot = (rope_rotate(q_sum, lengths) * head_dim ** -0.5).astype(jnp.bfloat16)
        k_new = rope_rotate(k_sum, lengths).astype(jnp.bfloat16)
        v_new = v_sum.astype(jnp.bfloat16)
        attn_out, k_upd, v_upd = attend(q_rot, k_cache, v_cache, k_new, v_new, lengths)
        attn_rows = lax.all_gather(attn_out.reshape(row_count, head_count * head_dim), 'dm', axis=0, tiled=True)
        attn_proj = lax.psum(jnp.dot(attn_rows, w_o, preferred_element_type=jnp.float32), 'tp')
        mid_f = (resid_f + attn_proj).astype(jnp.bfloat16).astype(jnp.float32)
        normed_mlp = width_norm(mid_f, norm_mlp)
        gate_val = lax.psum(jnp.dot(normed_mlp, w_gate, preferred_element_type=jnp.float32), 'dm')
        up_val = lax.psum(jnp.dot(normed_mlp, w_up, preferred_element_type=jnp.float32), 'dm')
        hidden = (jax.nn.gelu(gate_val, approximate=True) * up_val).astype(jnp.bfloat16)
        down_sum = lax.psum(jnp.dot(hidden, w_down, preferred_element_type=jnp.float32), 'tp')
        resid_out = (mid_f + down_sum).astype(jnp.bfloat16)
        return resid_out, k_upd, v_upd

    return jax.shard_map(local_step, mesh=mesh, in_specs=in_specs, out_specs=out_specs, check_vma=False)
```

profile of v0, /device:TPU:1, one launch (start us, length us, event | category | flops | bytes accessed | tf_op | source)
XLA Modules:
  0.0 578.1 jit_solution(4708562615461985)
XLA Ops:
  7.2 0.0 copy-start
  7.2 0.0 reduce-scatter.6.cloned.1.call-start
  7.2 0.8 convert_add_fusion.3
  8.0 1.6 fusion.11
  9.6 0.0 copy-start.2
  9.6 0.0 copy-start.6
  9.6 13.5 %psum.42 = f32[1536,1]{0,1:T(1,128)S(1)} all-reduce(f32[1536,1]{0,1:T(1,128)S(1)} %broadcast_in_dim.31), channel_id=1, replica_groups=mesh['dp'=1,'tp'=16,'dm'=8] {'dm'}, use_global_device_ids=true, to_apply=%region_1.0 | all-reduce | flops 1536 | bytes 12288 | tf_op jit(solution)/shard_map/psum | solution.py:52
  23.2 3.0 fusion.59
  26.2 0.0 reduce-scatter.6.cloned.1.call-update
  26.3 0.0 copy-start.7
  26.3 0.0 reduce-scatter.4.cloned.1.call-start
  26.3 0.0 copy-done.2
  26.3 0.0 copy-done.6
  26.3 1.8 fusion.61
  28.1 0.0 reduce-scatter.4.cloned.1.call-update
  28.1 0.0 reduce-scatter.8.cloned.1.call-start
  28.2 0.0 copy-done.7
  28.2 1.8 fusion.57
  30.0 0.0 reduce-scatter.8.cloned.1.call-update
  30.0 0.0 all-reduce.5.cloned.1.call-start
  30.1 0.8 fusion.64
  30.8 0.1 iota_compare_fusion
  30.9 27.9 %reduce-scatter.6.cloned.1.call-done = f32[192,256]{1,0:T(8,128)} async-done(((f32[1536,256]{1,0:T(8,128)}), f32[192,256]{1,0:T(8,128)}) %reduce-scatter.6.cloned.1.call-update) | async-done | bytes 196624 | tf_op jit(solution)/shard_map/reduce_scatter | solution.py:57
  58.8 34.8 %reduce-scatter.4.cloned.1.call-done = f32[192,256]{1,0:T(8,128)} async-done(((f32[1536,256]{1,0:T(8,128)}), f32[192,256]{1,0:T(8,128)}) %reduce-scatter.4.cloned.1.call-update) | async-done | bytes 196624 | tf_op jit(solution)/shard_map/reduce_scatter | solution.py:57
  93.7 1.5 fusion.38
  95.2 32.7 %reduce-scatter.8.cloned.1.call-done = f32[192,256]{1,0:T(8,128)} async-done(((f32[1536,256]{1,0:T(8,128)}), f32[192,256]{1,0:T(8,128)}) %reduce-scatter.8.cloned.1.call-update) | async-done | bytes 196624 | tf_op jit(solution)/shard_map/reduce_scatter | solution.py:57
  127.9 0.9 convert_element_type.62
  128.9 2.2 broadcast_select_fusion.1
  131.0 0.0 copy-start.3
  131.0 0.0 copy-start.4
  131.1 0.0 copy-start.8
  131.1 0.5 fusion.21
  131.6 0.2 fusion.48
  131.8 0.2 fusion.49
  132.0 0.2 fusion.50
  132.2 0.4 fusion.19
  132.6 0.0 copy-done.3
  132.6 0.1 copy-done.4
  132.7 16.6 %all_gather.3 = bf16[1536,256]{1,0:T(8,128)(2,1)S(1)} all-gather(bf16[192,256]{1,0:T(8,128)(2,1)S(1)} %bitcast.36), channel_id=1, replica_groups=mesh['dp'=1,'tp'=16,'dm'=8] {'dm'}, dimensions={0}, use_global_device_ids=true | all-gather | bytes 884736 | tf_op jit(solution)/shard_map/all_gather | solution.py:69
  149.3 0.0 copy-done.8
  149.3 0.0 copy-start.9
  149.3 2.0 fusion.65
  151.3 0.0 all-reduce.5.cloned.1.call-update
  151.3 0.0 all-reduce.9.cloned.1.call-start
  151.3 0.0 copy-done.9
  151.4 90.0 %all-reduce.5.cloned.1.call-done = f32[1536,384]{1,0:T(8,128)} async-done(((f32[1536,384]{1,0:T(8,128)}), f32[1536,384]{1,0:T(8,128)}) %all-reduce.5.cloned.1.call-update) | async-done | bytes 2359312 | tf_op jit(solution)/shard_map/psum | solution.py:70
  241.4 2.1 fusion.15
  243.5 14.0 %psum.44 = f32[1536,1]{0,1:T(1,128)S(1)} all-reduce(f32[1536,1]{0,1:T(1,128)S(1)} %broadcast_in_dim.60), channel_id=1, replica_groups=mesh['dp'=1,'tp'=16,'dm'=8] {'dm'}, use_global_device_ids=true, to_apply=%region_9.10 | all-reduce | flops 1536 | bytes 12288 | tf_op jit(solution)/shard_map/psum | solution.py:52
  257.5 0.0 copy-done
  257.5 0.0 copy-start.5
  257.6 5.4 fusion.23
  262.9 0.0 copy-done.5
  262.9 5.3 fusion.25
  268.2 0.0 copy-start.10
  268.2 0.0 all-reduce.9.cloned.1.call-update
  268.2 0.0 all-reduce.7.cloned.1.call-start
  268.3 199.2 %all-reduce.9.cloned.1.call-done = (f32[1536,1536]{1,0:T(8,128)}, f32[1536,1536]{1,0:T(8,128)}) async-done(((f32[1536,1536]{1,0:T(8,128)}, f32[1536,1536]{1,0:T(8,128)}), (f32[1536,1536]{1,0:T(8,128)}, f32[1536,1536]{1,0:T(8,128)})) %all-reduce.9.cloned.1.call-update) | async-done | bytes 18874384 | tf_op jit(solution)/shard_map/psum | solution.py:74
  467.5 0.0 copy-done.10
  467.5 9.8 %fusion.9 = f32[1536,384]{1,0:T(8,128)} fusion(bf16[1536,384]{1,0:T(8,128)(2,1)S(1)} %copy-done.10, f32[1536,1536]{1,0:T(8,128)} %get-tuple-element.3, f32[1536,1536]{1,0:T(8,128)} %get-tuple-element.4), kind=kOutput, calls=%fused_computation.10 | convolution fusion | flops 1835532288 | bytes 22413312 | tf_op jit(solution)/shard_map/dot_general | solution.py:76
  477.3 0.0 all-reduce.7.cloned.1.call-update
  477.4 0.0 copy-start.1
  477.4 91.0 %all-reduce.7.cloned.1.call-done = f32[1536,384]{1,0:T(8,128)} async-done(((f32[1536,384]{1,0:T(8,128)}), f32[1536,384]{1,0:T(8,128)}) %all-reduce.7.cloned.1.call-update) | async-done | bytes 2359312 | tf_op jit(solution)/shard_map/psum | solution.py:76
  568.3 2.9 fusion.18
  571.2 0.0 copy-done.1
  (9 shorter events, 0.1 us)
Async XLA Ops:
  7.2 250.4 %copy-start = (bf16[384,1536]{1,0:T(8,128)(2,1)S(1)}, bf16[384,1536]{1,0:T(8,128)(2,1)}, u32[]{:S(2)}) copy-start(bf16[384,1536]{1,0:T(8,128)(2,1)} %param.24) | copy-start | bytes 3538948
  7.2 51.7 %reduce-scatter.6.cloned.1.call-start = ((), (), s32[]{:S(2)}) async-start(), calls=%async_computation.4 | async-start | bytes 1769472 | tf_op jit(solution)/shard_map/reduce_scatter | solution.py:57
  9.6 16.8 %copy-start.2 = (bf16[1536,384]{1,0:T(8,128)(2,1)S(1)}, bf16[1536,384]{1,0:T(8,128)(2,1)}, u32[]{:S(2)}) copy-start(bf16[1536,384]{1,0:T(8,128)(2,1)} %param.13) | copy-start | bytes 3538948
  9.6 16.7 %copy-start.6 = (bf16[384,256]{1,0:T(8,128)(2,1)S(1)}, bf16[384,256]{1,0:T(8,128)(2,1)}, u32[]{:S(2)}) copy-start(bf16[384,256]{1,0:T(8,128)(2,1)} %param.18) | copy-start | bytes 589828
  26.3 1.9 copy-start.7
  26.3 67.4 %reduce-scatter.4.cloned.1.call-start = ((), (), s32[]{:S(2)}) async-start(), calls=%async_computation.3 | async-start | bytes 1769472 | tf_op jit(solution)/shard_map/reduce_scatter | solution.py:57
  28.1 99.8 %reduce-scatter.8.cloned.1.call-start = ((), (), s32[]{:S(2)}) async-start(), calls=%async_computation.5 | async-start | bytes 1769472 | tf_op jit(solution)/shard_map/reduce_scatter | solution.py:57
  30.0 211.4 %all-reduce.5.cloned.1.call-start = ((), (), s32[]{:S(2)}) async-start(), calls=%async_computation.6 | async-start | bytes 4718592 | tf_op jit(solution)/shard_map/psum | solution.py:70
  131.0 1.5 copy-start.3
  131.0 1.7 copy-start.4
  131.1 18.2 %copy-start.8 = (bf16[256,384]{1,0:T(8,128)(2,1)S(1)}, bf16[256,384]{1,0:T(8,128)(2,1)}, u32[]{:S(2)}) copy-start(bf16[256,384]{1,0:T(8,128)(2,1)} %param.21) | copy-start | bytes 589828
  149.3 2.0 copy-start.9
  151.3 316.2 %all-reduce.9.cloned.1.call-start = ((), (), s32[]{:S(2)}) async-start(), calls=%async_computation.8 | async-start | bytes 37748736 | tf_op jit(solution)/shard_map/psum | solution.py:74
  257.5 5.4 copy-start.5
  268.2 199.3 %copy-start.10 = (bf16[1536,384]{1,0:T(8,128)(2,1)S(1)}, bf16[1536,384]{1,0:T(8,128)(2,1)}, u32[]{:S(2)}) copy-start(bf16[1536,384]{1,0:T(8,128)(2,1)} %param.25) | copy-start | bytes 3538948
  268.2 300.1 %all-reduce.7.cloned.1.call-start = ((), (), s32[]{:S(2)}) async-start(), calls=%async_computation.7 | async-start | bytes 4718592 | tf_op jit(solution)/shard_map/psum | solution.py:76
  477.4 93.9 %copy-start.1 = (bf16[384,1536]{1,0:T(8,128)(2,1)S(1)}, bf16[384,1536]{1,0:T(8,128)(2,1)}, u32[]{:S(2)}) copy-start(bf16[384,1536]{1,0:T(8,128)(2,1)} %param.24) | copy-start | bytes 3538948
Sparse Core Ops, SparseCore 0:
  26.4 32.4 reduce-scatter.5
  61.8 31.7 reduce-scatter.3
  96.1 31.7 reduce-scatter.7
  151.4 89.9 all-reduce.4
  268.4 199.0 all-reduce.8
  477.5 90.7 all-reduce.6
where the time goes:
time: 579 us; the launch traced here: 578 us
  waiting for transfers between devices  476 us (82%)
  blocking collectives  44.2 us (8%)
  matrix products  29.9 us (5%)
  between operations  14.4 us (2%)
  other arithmetic  13.5 us (2%)
    psum x1, waiting for transfers between devices, local_step(): lax.psum(jnp.dot(normed_mlp, w_up, preferred_element_type=jnp.float32), '...  199 us
    reduce_scatter x3, waiting for transfers between devices, row_sum(): lax.psum_scatter(partial_val, 'dm', scatter_dimension=0, tiled=True)  95.4 us
    psum x1, waiting for transfers between devices, local_step(): lax.psum(jnp.dot(hidden, w_down, preferred_element_type=jnp.float32), 'tp')  91 us
    psum x1, waiting for transfers between devices, local_step(): lax.psum(jnp.dot(attn_rows, w_o, preferred_element_type=jnp.float32), 'tp')  90 us
    psum x2, blocking collectives, width_norm(): sq_total = lax.psum(jnp.sum(rows_f * rows_f, axis=1, keepdims=True), 'dm')  27.6 us
    all_gather x1, blocking collectives, local_step(): lax.all_gather(attn_out.reshape(row_count, head_count * head_dim), 'dm',...  16.6 us
  transfers between devices with their start and end apart: 6, of which 6 were waited for; matrix products, arithmetic and copies ran while one was open for 1% of the time, Pallas kernels for 0%

commit v1 on v0

v1 whole, which is shorter than its diff:
```python
import functools

import jax
import jax.numpy as jnp
from jax import lax
from jax.experimental import pallas as pl
from jax.experimental.pallas import tpu as pltpu
from jax.sharding import PartitionSpec as P

EPSILON = 1e-6
ROPE_THETA = 10000.0
BF = jnp.bfloat16
F32 = jnp.float32
LOGICAL = pl.DeviceIdType.LOGICAL


class Comm:
    def __init__(self, ssem, rsem):
        self.ssem, self.rsem, self.n, self.copies = ssem, rsem, 0, []
        tp, dm = lax.axis_index('tp'), lax.axis_index('dm')
        self.tp, self.dm = tp, dm
        self.z, self.y = lax.div(tp, 4), lax.rem(tp, 4)
        self.x, self.c = lax.div(dm, 2), lax.rem(dm, 2)

    def ring(self, axis):
        i = {'x': self.x, 'y': self.y, 'z': self.z}[axis]
        idx = [lax.rem(i + k, 4) for k in range(4)]
        dev = [self.at(axis, j) for j in idx]
        return idx, dev

    def at(self, axis, j):
        if axis == 'x':
            return self.tp * 8 + j * 2 + self.c
        if axis == 'y':
            return (self.z * 4 + j) * 8 + self.dm
        return (j * 4 + self.y) * 8 + self.dm

    def other(self):
        return self.tp * 8 + self.x * 2 + 1 - self.c

    def barrier(self, peers):
        sem = pltpu.get_barrier_semaphore()
        for dev in peers:
            pl.semaphore_signal(sem, inc=1, device_id=dev, device_id_type=LOGICAL)
        pl.semaphore_wait(sem, len(peers))

    def send(self, src, dst, dev):
        k = self.n
        self.n += 1
        copy = pltpu.make_async_remote_copy(src_ref=src, dst_ref=dst, send_sem=self.ssem.at[k], recv_sem=self.rsem.at[k], device_id=dev, device_id_type=LOGICAL)
        copy.start()
        self.copies.append(copy)
        return copy

    def drain(self):
        for copy in self.copies:
            copy.wait_send()


def run(*gens):
    gens = list(gens)
    while gens:
        for g in list(gens):
            try:
                next(g)
            except StopIteration:
                gens.remove(g)


def gather4(cm, axis, blk, hf, own=None):
    (i, r, o, l), (_, dr, _, dl) = cm.ring(axis)
    own = blk(i) if own is None else own
    a = cm.send(own, blk(i), dr)
    b = cm.send(own, blk(i), dl)
    yield
    a.wait_recv()
    c = cm.send(hf(l, 0), hf(l, 0), dr)
    b.wait_recv()
    d = cm.send(hf(r, 1), hf(r, 1), dl)
    yield
    c.wait_recv()
    d.wait_recv()


def scatter4(cm, axis, blk, hf, ro0, ro1, rl, rr, hrx):
    (i, r, o, l), (_, dr, _, dl) = cm.ring(axis)
    c0 = cm.send(hf(o, 0), ro0, dr)
    c1 = cm.send(hf(o, 1), ro1, dl)
    c2 = cm.send(hf(r, 1), hrx(rl, 1), dr)
    c3 = cm.send(hf(l, 0), hrx(rr, 0), dl)
    yield
    c0.wait_recv()
    hf(r, 0)[...] += ro0[...]
    c4 = cm.send(hf(r, 0), hrx(rl, 0), dr)
    c1.wait_recv()
    hf(l, 1)[...] += ro1[...]
    c5 = cm.send(hf(l, 1), hrx(rr, 1), dl)
    yield
    for c in (c2, c3, c4, c5):
        c.wait_recv()
    blk(i)[...] += rl[...] + rr[...]


def plane_scatter(cm, p, h, rx):
    ro, rb, so, sb = rx
    ph = p.at[h]
    if h == 0:
        big = lambda j: ph.at[:, j]
        bigh = lambda j, s: ph.at[2 * s:2 * s + 2, j]
        small = lambda j: ph.at[j, cm.y]
        smallh = lambda j, s: ph.at[j, cm.y, 24 * s:24 * s + 24]
        axes = ('y', 'z')
    else:
        big = lambda j: ph.at[j]
        bigh = lambda j, s: ph.at[j, 2 * s:2 * s + 2]
        small = lambda j: ph.at[cm.z, j]
        smallh = lambda j, s: ph.at[cm.z, j, 24 * s:24 * s + 24]
        axes = ('z', 'y')
    yield from scatter4(cm, axes[0], big, bigh, ro.at[h, 0], ro.at[h, 1], rb.at[h, 0], rb.at[h, 1], lambda b, s: b.at[2 * s:2 * s + 2])
    yield from scatter4(cm, axes[1], small, smallh, so.at[h, 0], so.at[h, 1], sb.at[h, 0], sb.at[h, 1], lambda b, s: b.at[24 * s:24 * s + 24])


def plane_gather(cm, m, h, split):
    mh = m.at[h]
    cols = m.shape[-1]
    cut = lambda s: pl.ds(0, split) if s == 0 else pl.ds(split, cols - split)
    if h == 0:
        yield from gather4(cm, 'y', lambda j: mh.at[cm.z, j], lambda j, s: mh.at[cm.z, j, :, cut(s)])
        yield from gather4(cm, 'z', lambda j: mh.at[j], lambda j, s: mh.at[j, 2 * s:2 * s + 2])
    else:
        yield from gather4(cm, 'z', lambda j: mh.at[j, cm.y], lambda j, s: mh.at[j, cm.y, :, cut(s)])
        yield from gather4(cm, 'y', lambda j: mh.at[:, j], lambda j, s: mh.at[2 * s:2 * s + 2, j])


def gain_row(g_ref, d, k):
    g = g_ref[d]
    return jnp.concatenate([g[3 * k + j:3 * k + j + 1] for j in range(3)], axis=1)


def qkv_kernel(x_ref, wq_ref, wk_ref, wv_ref, gain_ref, q_ref, k_ref, v_ref, g_ref, w_buf, xg, n_buf, ssem, rsem):
    cm = Comm(ssem, rsem)
    x, c, dm = cm.x, cm.c, cm.dm
    ring_y, ring_z, ring_x = cm.ring('y'), cm.ring('z'), cm.ring('x')
    peers = [cm.tp * 8 + lax.rem(dm + k, 8) for k in range(1, 8)]
    plane = [ring_y[1][1], ring_y[1][3], ring_z[1][1], ring_z[1][3]]
    cm.barrier(peers + plane)

    sl = jnp.where(c == 0, cm.y, cm.z)
    xs = []
    for k, dev in enumerate(peers):
        start = pl.multiple_of(lax.rem(dm + k + 1, 8) * 192 + sl * 48, 16)
        xs.append(cm.send(x_ref.at[pl.ds(start, 48), :], xg.at[c, sl, x], dev))
    gs = [cm.send(gain_ref, g_ref.at[dm], dev) for dev in peers]
    (i, r, o, l), (_, dr, _, dl) = ring_x
    dev_o = cm.other()
    rows = lambda j: w_buf.at[j * 2 + c]
    ws = (wq_ref, wk_ref, wv_ref)
    a = [cm.send(w, rows(i).at[n], dr) for n, w in enumerate(ws)]
    b = [cm.send(w, rows(i).at[n], dl) for n, w in enumerate(ws)]
    e = [cm.send(w, rows(i).at[n], dev_o) for n, w in enumerate(ws)]
    for n, w in enumerate(ws):
        w_buf[dm, n] = w[...]
    g_ref[dm] = gain_ref[...]
    own = pl.multiple_of(dm * 192 + sl * 48, 16)
    xg[c, sl, x] = x_ref[pl.ds(own, 48), :]
    for cp in xs:
        cp.wait_recv()

    def w_ring():
        yield
        yield
        for cp in a:
            cp.wait_recv()
        f0 = cm.send(rows(l).at[:, 0:192], rows(l).at[:, 0:192], dr)
        e1 = cm.send(rows(l), rows(l), dev_o)
        for cp in b:
            cp.wait_recv()
        f1 = cm.send(rows(r).at[:, 192:384], rows(r).at[:, 192:384], dl)
        e2 = cm.send(rows(r), rows(r), dev_o)
        yield
        f0.wait_recv()
        f1.wait_recv()
        e3 = cm.send(rows(o), rows(o), dev_o)
        for cp in e + [e1, e2, e3]:
            cp.wait_recv()

    gy = gather4(cm, 'y', lambda j: xg.at[0, j], lambda j, s: xg.at[0, j, 2 * s:2 * s + 2])
    gz = gather4(cm, 'z', lambda j: xg.at[1, j], lambda j, s: xg.at[1, j, 2 * s:2 * s + 2])
    run(gy, gz, w_ring())
    for cp in gs:
        cp.wait_recv()

    total = jnp.zeros((192, 1), F32)
    for d in range(8):
        v = xg[d % 2, :, d // 2].reshape(192, 384).astype(F32)
        total += jnp.sum(v * v, axis=1, keepdims=True)
    inv = lax.rsqrt(total / 3072 + EPSILON)
    for d in range(8):
        v = xg[d % 2, :, d // 2].reshape(192, 384).astype(F32)
        n_buf[d] = (v * inv * (1.0 + gain_row(g_ref, d, 0))).astype(BF)
    for n, out in enumerate((q_ref, k_ref, v_ref)):
        acc = jnp.zeros((192, 256), F32)
        for d in range(8):
            acc += jnp.dot(n_buf[d], w_buf[d, n], preferred_element_type=F32)
        out[...] = acc
    cm.drain()


def proj_kernel(o_ref, x_ref, wo_ref, wg_ref, wu_ref, g_ref, m_buf, w_gu, h_ref, o_buf, wo_o, x_o, p1, ro, rb, so, sb, hs, t0, t1, ssem, rsem):
    cm = Comm(ssem, rsem)
    x, c, dm, y, z = cm.x, cm.c, cm.dm, cm.y, cm.z
    (_, r, o, l), (_, dr, _, dl) = cm.ring('x')
    ring_y, ring_z = cm.ring('y'), cm.ring('z')
    dev_o = cm.other()
    cm.barrier([dev_o, dr, dl, ring_y[1][1], ring_y[1][3], ring_z[1][1], ring_z[1][3]])

    ro_0, ro_1 = ro, so
    go = gather4(cm, 'x', lambda j: o_buf.at[j], lambda j, s: o_buf.at[j, 96 * s:96 * s + 96], own=o_ref)
    next(go)
    o_buf[x] = o_ref[...]
    row = lambda core: pl.multiple_of(192 * (2 * z + core) + 48 * y, 16)
    c_wo = cm.send(wo_ref, wo_o, dev_o)
    c_x = cm.send(x_ref.at[pl.ds(row(1 - c), 48), :], x_o, dev_o)
    for _ in go:
        pass
    kblk = lambda j, core: pl.ds(pl.multiple_of((j * 2 + core) * 384, 16), 384)
    hcol = lambda j: pl.ds(pl.multiple_of(j * 384, 128), 384)
    c_t0 = cm.send(wg_ref.at[:, hcol(o)], t0, dr)
    c_t1 = cm.send(wu_ref.at[:, hcol(o)], t1, dl)
    c_gr = cm.send(wg_ref.at[:, hcol(r)], w_gu.at[kblk(x, c), 0:384], dr)
    c_gl = cm.send(wg_ref.at[:, hcol(l)], w_gu.at[kblk(x, c), 0:384], dl)
    c_ur = cm.send(wu_ref.at[:, hcol(r)], w_gu.at[kblk(x, c), 384:768], dr)
    c_ul = cm.send(wu_ref.at[:, hcol(l)], w_gu.at[kblk(x, c), 384:768], dl)
    c_og = cm.send(wg_ref.at[:, hcol(x)], w_gu.at[kblk(x, c), 0:384], dev_o)
    c_ou = cm.send(wu_ref.at[:, hcol(x)], w_gu.at[kblk(x, c), 384:768], dev_o)
    w_gu[kblk(x, c), 0:384] = wg_ref[:, hcol(x)]
    w_gu[kblk(x, c), 384:768] = wu_ref[:, hcol(x)]

    c_wo.wait_recv()

    def o_proj(j, carry):
        v = o_buf[j]
        p1[c, j] = jnp.dot(v, wo_ref[...], preferred_element_type=F32).reshape(4, 48, 384)
        p1[1 - c, j] = jnp.dot(v, wo_o[...], preferred_element_type=F32).reshape(4, 48, 384)
        return carry

    lax.fori_loop(0, 4, o_proj, 0)

    def w_deal():
        yield
        yield
        yield
        c_t0.wait_recv()
        f0 = cm.send(t0, w_gu.at[kblk(l, c), 0:384], dr)
        c_t1.wait_recv()
        f1 = cm.send(t1, w_gu.at[kblk(r, c), 384:768], dl)
        yield
        c_gr.wait_recv()
        c_ur.wait_recv()
        e1 = cm.send(w_gu.at[kblk(l, c)], w_gu.at[kblk(l, c)], dev_o)
        c_gl.wait_recv()
        c_ul.wait_recv()
        e2 = cm.send(w_gu.at[kblk(r, c)], w_gu.at[kblk(r, c)], dev_o)
        deal.extend([f0, f1, e1, e2])

    deal = []
    run(plane_scatter(cm, p1, 0, (ro, rb, so, sb)), plane_scatter(cm, p1, 1, (ro, rb, so, sb)), w_deal())

    c_x.wait_recv()
    hs[x, c] = (x_ref[pl.ds(row(c), 48), :].astype(F32) + p1[c, z, y]).astype(BF)
    hs[x, 1 - c] = (x_o[...].astype(F32) + p1[1 - c, z, y]).astype(BF)
    run(gather4(cm, 'x', lambda j: hs.at[j], lambda j, s: hs.at[j, s]))
    total = jnp.zeros((48, 1), F32)
    for d in range(8):
        v = hs[d // 2, d % 2].astype(F32)
        total += jnp.sum(v * v, axis=1, keepdims=True)
    inv = lax.rsqrt(total / 3072 + EPSILON)
    for d in range(8):
        v = hs[d // 2, d % 2].astype(F32)
        m_buf[d // 4, z, y, :, 384 * (d % 4):384 * (d % 4) + 384] = (v * inv * (1.0 + gain_row(g_ref, d, 1))).astype(BF)

    def w_last():
        f0, f1, e1, e2 = deal
        yield
        f0.wait_recv()
        f1.wait_recv()
        e3 = cm.send(w_gu.at[kblk(o, c)], w_gu.at[kblk(o, c)], dev_o)
        yield
        for cp in (c_og, c_ou, e1, e2, e3):
            cp.wait_recv()

    run(plane_gather(cm, m_buf, 0, 768), plane_gather(cm, m_buf, 1, 768), w_last())
    h_ref[...] = hs[x]
    cm.drain()


def mlp_kernel(m_buf, w_gu, h_ref, wd_ref, out_ref, wd_o, p2, ro, rb, so, sb, a_buf, u_buf, v_buf, ssem, rsem):
    cm = Comm(ssem, rsem)
    x, c, dm, y, z = cm.x, cm.c, cm.dm, cm.y, cm.z
    (_, r, o, l), (_, dr, _, dl) = cm.ring('x')
    ring_y, ring_z = cm.ring('y'), cm.ring('z')
    dev_o = cm.other()
    cm.barrier([dev_o, dr, dl, ring_y[1][1], ring_y[1][3], ring_z[1][1], ring_z[1][3]])
    hcol = lambda j: pl.ds(pl.multiple_of(j * 384, 128), 384)
    c_wd = cm.send(wd_ref, wd_o, dev_o)

    def gate_up(j, carry):
        m0 = m_buf[0, j].reshape(192, 1536)
        m1 = m_buf[1, j].reshape(192, 1536)
        acc = jnp.dot(m0, w_gu[0:1536], preferred_element_type=F32) + jnp.dot(m1, w_gu[1536:3072], preferred_element_type=F32)
        gate, up = acc[:, 0:384], acc[:, 384:768]
        a_buf[j, :, hcol(x)] = (0.5 * gate * (1.0 + jnp.tanh(0.7978845608 * (gate + 0.044715 * (gate * gate * gate)))) * up).astype(BF)
        return carry

    lax.fori_loop(0, 4, gate_up, 0)
    run(gather4(cm, 'x', lambda j: a_buf.at[:, :, hcol(j)], lambda j, s: a_buf.at[2 * s:2 * s + 2, :, hcol(j)]))
    c_wd.wait_recv()

    def down(j, carry):
        v = a_buf[j]
        p2[c, j] = jnp.dot(v, wd_ref[...], preferred_element_type=F32).reshape(4, 48, 384)
        p2[1 - c, j] = jnp.dot(v, wd_o[...], preferred_element_type=F32).reshape(4, 48, 384)
        return carry

    lax.fori_loop(0, 4, down, 0)
    run(plane_scatter(cm, p2, 0, (ro, rb, so, sb)), plane_scatter(cm, p2, 1, (ro, rb, so, sb)))
    for h in range(2):
        u_buf[h, z, y] = (h_ref[h].astype(F32) + p2[h, z, y]).astype(BF)
    run(plane_gather(cm, u_buf, 0, 256), plane_gather(cm, u_buf, 1, 256))
    c_v = cm.send(u_buf.at[1 - c], v_buf, dev_o)
    blk = lambda j, core: pl.ds(pl.multiple_of(192 * (2 * j + core), 16), 192)
    for j in range(4):
        out_ref[blk(j, c), :] = u_buf[c, j].reshape(192, 384)
    c_v.wait_recv()
    for j in range(4):
        out_ref[blk(j, 1 - c), :] = v_buf[j].reshape(192, 384)
    cm.drain()


def rope_rotate(vectors, positions):
    half_dim = vectors.shape[-1] // 2
    inv_freq = ROPE_THETA ** (-2.0 * jnp.arange(half_dim, dtype=jnp.float32) / vectors.shape[-1])
    angles = positions.astype(jnp.float32)[:, None] * inv_freq[None, :]
    cos_part = jnp.cos(angles)[:, None, :]
    sin_part = jnp.sin(angles)[:, None, :]
    first_half = vectors[..., :half_dim]
    second_half = vectors[..., half_dim:]
    return jnp.concatenate([first_half * cos_part - second_half * sin_part, second_half * cos_part + first_half * sin_part], axis=-1)


def attend(q_rot, k_cache, v_cache, k_new, v_new, lengths):
    slot_ids = jnp.arange(k_cache.shape[2])
    slot_hit = slot_ids[None, :] == lengths[:, None]
    valid_mask = slot_ids[None, :] <= lengths[:, None]
    k_upd = jnp.where(slot_hit[:, None, :, None], k_new[:, :, None, :], k_cache)
    v_upd = jnp.where(slot_hit[:, None, :, None], v_new[:, :, None, :], v_cache)
    scores = jnp.einsum('bhe,bhte->bht', q_rot, k_upd, preferred_element_type=jnp.float32)
    scores = jnp.where(valid_mask[:, None, :], scores, -1e30)
    attn_probs = jax.nn.softmax(scores, axis=-1).astype(jnp.bfloat16)
    attn_out = jnp.einsum('bht,bhte->bhe', attn_probs, v_upd, preferred_element_type=jnp.float32)
    return attn_out.astype(jnp.bfloat16), k_upd, v_upd


VM = pl.BlockSpec(memory_space=pltpu.VMEM)
VMEM_LIMIT = 60 * 1024 * 1024


def call(body, outs, scratch, sems, cid, flops, *args):
    single = len(outs) == 1
    return pl.pallas_call(
        body,
        out_shape=outs[0] if single else outs,
        in_specs=[VM] * len(args),
        out_specs=VM if single else [VM] * len(outs),
        scratch_shapes=scratch + [pltpu.SemaphoreType.DMA((sems,)), pltpu.SemaphoreType.DMA((sems,))],
        compiler_params=pltpu.CompilerParams(collective_id=cid, has_side_effects=True, vmem_limit_bytes=VMEM_LIMIT),
        cost_estimate=pl.CostEstimate(flops=flops, bytes_accessed=8_000_000, transcendentals=0),
    )(*args)


def call2(body, outs, scratch, sems, cid, flops, *args):
    single = len(outs) == 1
    return pl.pallas_call(
        body,
        out_shape=outs[0] if single else outs,
        in_specs=[VM] * len(args),
        out_specs=VM if single else [VM] * len(outs),
        scratch_shapes=scratch + [pltpu.SemaphoreType.DMA((sems,)), pltpu.SemaphoreType.DMA((sems,))],
        compiler_params=pltpu.CompilerParams(collective_id=cid, has_side_effects=True, vmem_limit_bytes=VMEM_LIMIT),
        cost_estimate=pl.CostEstimate(flops=flops, bytes_accessed=8_000_000, transcendentals=0),
    )(*args)


def call3(body, outs, scratch, sems, cid, flops, *args):
    single = len(outs) == 1
    return pl.pallas_call(
        body,
        out_shape=outs[0] if single else outs,
        in_specs=[VM] * len(args),
        out_specs=VM if single else [VM] * len(outs),
        scratch_shapes=scratch + [pltpu.SemaphoreType.DMA((sems,)), pltpu.SemaphoreType.DMA((sems,))],
        compiler_params=pltpu.CompilerParams(collective_id=cid, has_side_effects=True, vmem_limit_bytes=VMEM_LIMIT),
        cost_estimate=pl.CostEstimate(flops=flops, bytes_accessed=8_000_000, transcendentals=0),
    )(*args)


def solution(mesh):
    cache_spec = P(('dp', 'dm'), 'tp', None, None)
    resid_spec = P('dp', 'dm')
    col_spec = P('dm', 'tp')
    row_spec = P('tp', 'dm')
    in_specs = (resid_spec, cache_spec, cache_spec, P('dp'), P('dm'), col_spec, col_spec, col_spec, row_spec, P('dm'), col_spec, col_spec, row_spec)
    out_specs = (resid_spec, cache_spec, cache_spec)
    sds = jax.ShapeDtypeStruct
    V = pltpu.VMEM

    def local_step(resid_in, k_cache, v_cache, cache_len, norm_attn, w_q, w_k, w_v, w_o, norm_mlp, w_gate, w_up, w_down):
        lengths = lax.dynamic_slice_in_dim(cache_len, lax.axis_index('dm') * 192, 192)
        gains = jnp.concatenate([norm_attn.reshape(3, 128), norm_mlp.reshape(3, 128), jnp.zeros((2, 128), BF)]).astype(F32)
        q_sum, k_sum, v_sum, gain_all = call(
            qkv_kernel,
            (sds((192, 256), F32),) * 3 + (sds((8, 8, 128), F32),),
            [V((8, 3, 384, 256), BF), V((2, 4, 4, 48, 384), BF), V((8, 192, 384), BF)],
            40, 0, 2 * 10**9,
            resid_in, w_q, w_k, w_v, gains)
        heads = lambda a: a.reshape(192, 1, 256)
        q_rot = (rope_rotate(heads(q_sum), lengths) * 256 ** -0.5).astype(BF)
        k_new = rope_rotate(heads(k_sum), lengths).astype(BF)
        v_new = heads(v_sum).astype(BF)
        attn_out, k_upd, v_upd = attend(q_rot, k_cache, v_cache, k_new, v_new, lengths)
        rx = [V((2, 2, 2, 48, 384), F32), V((2, 2, 4, 48, 384), F32), V((2, 2, 24, 384), F32), V((2, 2, 48, 384), F32)]
        m_all, w_gu, h_own = call2(
            proj_kernel,
            (sds((2, 4, 4, 48, 1536), BF), sds((3072, 768), BF), sds((2, 48, 384), BF)),
            [V((4, 192, 256), BF), V((256, 384), BF), V((48, 384), BF), V((2, 4, 4, 48, 384), F32)] + rx + [V((4, 2, 48, 384), BF), V((384, 384), BF), V((384, 384), BF)],
            80, 1, 10**9,
            attn_out.reshape(192, 256), resid_in, w_o, w_gate, w_up, gain_all)
        resid_out = call3(
            mlp_kernel,
            (sds((1536, 384), BF),),
            [V((1536, 384), BF), V((2, 4, 4, 48, 384), F32)] + rx + [V((4, 192, 1536), BF), V((2, 4, 4, 48, 384), BF), V((4, 4, 48, 384), BF)],
            80, 2, 6 * 10**9,
            m_all, w_gu, h_own, w_down)
        return resid_out, k_upd, v_upd

    return jax.shard_map(local_step, mesh=mesh, in_specs=in_specs, out_specs=out_specs, check_vma=False)
```

time: 579 us -> 206 us (0.36)
  waiting for transfers between devices: 476 us -> 0 us
  Pallas kernels: 0 us -> 194 us
  blocking collectives: 44.2 us -> 0 us
  matrix products: 29.9 us -> 0.86 us
  between operations: 14.4 us -> 0.79 us
  other arithmetic: 13.5 us -> 5.98 us
    psum x3 -> x0, waiting for transfers between devices: 380 us -> none  [the longest x1 199 us: local_step(): lax.psum(jnp.dot(normed_mlp, w_up, preferred_element_type=jnp.float32), '...]
    pallas_call x0 -> x3, Pallas kernels: none -> 194 us  [the longest x1 80.1 us: call3(): pl.pallas_call(body, out_shape=outs[0] if single else outs, in_specs=[VM]...]
    reduce_scatter x3 -> x0, waiting for transfers between devices: 95.4 us -> none  [row_sum(): lax.psum_scatter(partial_val, 'dm', scatter_dimension=0, tiled=True)]
    dot_general x7 -> x0, matrix products: 29 us -> none  [the longest x1 9.83 us: local_step(): jnp.dot(hidden, w_down, preferred_element_type=jnp.float32)]
    psum x2 -> x0, blocking collectives: 27.6 us -> none  [width_norm(): sq_total = lax.psum(jnp.sum(rows_f * rows_f, axis=1, keepdims=True), 'dm')]
    all_gather x1 -> x0, blocking collectives: 16.6 us -> none  [local_step(): lax.all_gather(attn_out.reshape(row_count, head_count * head_dim), 'dm',...]
  transfers between devices with their start and end apart: 6 -> 0, of which waited for: 6 -> 0; matrix products, arithmetic and copies ran while one was open for 1% -> 0% of each run, Pallas kernels for 0% -> 0%
where the time goes in v1:
time: 206 us; the launch traced here: 205 us
  Pallas kernels  194 us (94%)
  other arithmetic  5.98 us (3%)
  local copies, waits for them, and re-layouts  3.32 us (2%)
    pallas_call x1, Pallas kernels, call3(): pl.pallas_call(body, out_shape=outs[0] if single else outs, in_specs=[VM]...  80.1 us
    pallas_call x1, Pallas kernels, call2(): pl.pallas_call(body, out_shape=outs[0] if single else outs, in_specs=[VM]...  75.1 us
    pallas_call x1, Pallas kernels, call(): pl.pallas_call(body, out_shape=outs[0] if single else outs, in_specs=[VM]...  38.6 us

profile of v1, /device:TPU:1, one launch (start us, length us, event | category | flops | bytes accessed | tf_op | source)
XLA Modules:
  0.0 204.8 jit_solution(11473200450813196311)
XLA Ops:
  0.6 0.1 pad.6.clone
  0.7 0.8 fusion.30
  1.5 1.4 maximum_convert_fusion.gain_ref
  2.9 0.1 iota_compare_fusion
  3.0 0.0 copy-start.1
  3.0 0.0 copy-start.2
  3.0 38.6 %shard_map.148 = (f32[192,256]{1,0:T(8,128)}, f32[192,256]{1,0:T(8,128)}, f32[192,256]{1,0:T(8,128)}, f32[8,8,128]{2,1,0:T(8,128)}) custom-call(bf16[1536,384]{1,0:T(8,128)(2,1)} %x_ref.3, bf16[384,256]{1,0:T(8,128)(2,1)} %wq_ref.1, bf16[384,256]{1,0:T(8,128)(2,1)} %wk_ref.1, bf16[384,256]{1,0:T(8,128)(2,1)} %wv_ref.1, f32[8,128]{1,0:T(8,128)} %maximum_convert_fusion.gain_ref), custom_call_target="tpu_custom_call" | custom-call | flops 2000000000 | bytes 8000000 | tf_op jit(solution)/shard_map/pallas_call | solution.py:370
  41.6 1.5 fusion.15
  43.2 0.9 convert_element_type.36
  44.1 0.0 copy-done.1
  44.1 0.0 copy-done.2
  44.1 0.7 broadcast_select_fusion.1
  44.8 0.0 copy-start
  44.8 0.0 copy-start.3
  44.9 0.5 fusion.2
  45.3 0.2 fusion.25
  45.6 0.2 fusion.26
  45.8 0.2 fusion.27
  45.9 0.4 fusion
  46.3 0.0 copy-done
  46.3 0.2 copy-done.3
  46.5 0.7 copy.25
  47.1 75.1 %shard_map.149 = (bf16[2,4,4,48,1536]{4,3,2,1,0:T(8,128)(2,1)}, bf16[3072,768]{1,0:T(8,128)(2,1)}, bf16[2,48,384]{2,1,0:T(8,128)(2,1)}) custom-call(bf16[192,256]{1,0:T(8,128)(2,1)} %bitcast.30, bf16[1536,384]{1,0:T(8,128)(2,1)} %x_ref.3, bf16[256,384]{1,0:T(8,128)(2,1)} %wo_ref.1, bf16[384,1536]{1,0:T(8,128)(2,1)} %wg_ref.1, bf16[384,1536]{1,0:T(8,128)(2,1)} %wu_ref.1, ...), custom_call_target="tpu_custom_call" | custom-call | flops 1000000000 | bytes 8000000 | tf_op jit(solution)/shard_map/pallas_call | solution.py:383
  122.3 80.1 %shard_map.150 = bf16[1536,384]{1,0:T(8,128)(2,1)} custom-call(bf16[2,4,4,48,1536]{4,3,2,1,0:T(8,128)(2,1)} %get-tuple-element.14.m_buf, bf16[3072,768]{1,0:T(8,128)(2,1)} %get-tuple-element.15.w_gu, bf16[2,48,384]{2,1,0:T(8,128)(2,1)} %get-tuple-element.16.h_ref, bf16[1536,384]{1,0:T(8,128)(2,1)} %wd_ref.1), custom_call_target="tpu_custom_call" | custom-call | flops 6000000000 | bytes 8000000 | tf_op jit(solution)/shard_map/pallas_call | solution.py:396
  202.4 2.4 %copy.27 = bf16[1536,384]{1,0:T(8,128)(2,1)} copy(bf16[1536,384]{1,0:T(8,128)(2,1)} %shard_map.150) | data formatting | bytes 2359296
  (4 shorter events, 0.0 us)
Async XLA Ops:
  3.0 41.1 %copy-start.1 = (bf16[192,1,16,256]{3,2,1,0:T(8,128)(2,1)S(1)}, bf16[192,1,16,256]{3,2,1,0:T(8,128)(2,1)}, u32[]{:S(2)}) copy-start(bf16[192,1,16,256]{3,2,1,0:T(8,128)(2,1)} %param.14) | copy-start | bytes 4718596
  3.0 41.1 %copy-start.2 = (bf16[192,1,16,256]{3,2,1,0:T(8,128)(2,1)S(1)}, bf16[192,1,16,256]{3,2,1,0:T(8,128)(2,1)}, u32[]{:S(2)}) copy-start(bf16[192,1,16,256]{3,2,1,0:T(8,128)(2,1)} %param.15) | copy-start | bytes 4718596
  44.8 1.5 copy-start
  44.8 1.7 copy-start.3
